TPU v7x, 8 devices: a whole 2x2x1 slice. The times are simulated.
8 devices in a mesh: dp: 1 (over z), pp: 2 (over y), tp: 4 (over x, core).
Axes of the slice: x: 2, y: 2, z: 1, core: 2. Of those that a mesh axis runs over, the one named last changes fastest.
Arguments:
- x_in: bfloat16 [64, 64, 2048], P('dp', 'tp')
- ln_gain: bfloat16 [2, 2, 2048], P(None, 'pp')
- w_in: bfloat16 [2, 2, 2048, 8192], P(None, 'pp', None, 'tp')
- w_out: bfloat16 [2, 2, 8192, 2048], P(None, 'pp', 'tp')
Outputs:
- output: bfloat16 [64, 64, 2048], P(('dp', 'pp'), 'tp')
All inputs are finite; a program needn't handle non-finite values.
Results may differ from a plain program's by a relative error of at most 0.0176923.
Values are sent between devices in bfloat16 or wider.
A program may use at most 1 GiB of HBM per device.

v0:
```python
import jax
import jax.numpy as jnp
from jax import lax
from jax.sharding import PartitionSpec as P

NORM_EPS = 1e-5


def layer_norm(resid, gain_vec):
    resid_f = resid.astype(jnp.float32)
    row_mean = jnp.mean(resid_f, axis=-1, keepdims=True)
    centred = resid_f - row_mean
    row_var = jnp.mean(centred * centred, axis=-1, keepdims=True)
    return (centred * lax.rsqrt(row_var + NORM_EPS) * gain_vec.astype(jnp.float32)).astype(jnp.bfloat16)


def solution(mesh):
    stages = mesh.shape["pp"]
    next_perm = [(src_stage, (src_stage + 1) % stages) for src_stage in range(stages)]

    def per_device(x_loc, gain_loc, w_in_loc, w_out_loc):
        micro_count, tok_shard = x_loc.shape[0], x_loc.shape[1]
        stage_idx = lax.axis_index("pp")
        rank_idx = lax.axis_index("tp")
        prev_stage = (stage_idx + stages - 1) % stages
        last_work = 2 * micro_count - 1

        def run_tick(tick_idx, loop_state):
            in_box, out_box = loop_state
            work_idx = tick_idx - stage_idx
            active = (work_idx >= 0) & (work_idx <= last_work)
            work_c = jnp.clip(work_idx, 0, last_work)
            virt_idx = work_c // micro_count
            micro_idx = work_c % micro_count
            gain_vec = lax.dynamic_index_in_dim(gain_loc, virt_idx, 0, keepdims=False)[0]
            w_first = lax.dynamic_index_in_dim(w_in_loc, virt_idx, 0, keepdims=False)[0]
            w_second = lax.dynamic_index_in_dim(w_out_loc, virt_idx, 0, keepdims=False)[0]
            cur_shard = lax.dynamic_index_in_dim(in_box, micro_idx, 0, keepdims=False)
            cur_full = lax.all_gather(cur_shard, "tp", axis=0, tiled=True)
            normed = layer_norm(cur_full, gain_vec)
            hidden = jax.nn.gelu(jnp.dot(normed, w_first, preferred_element_type=jnp.float32)).astype(jnp.bfloat16)
            part_prod = jnp.dot(hidden, w_second, preferred_element_type=jnp.float32).astype(jnp.bfloat16)
            reduced = lax.psum(part_prod, "tp")
            own_sum = lax.dynamic_slice_in_dim(reduced, rank_idx * tok_shard, tok_shard, axis=0)
            new_shard = (cur_shard.astype(jnp.float32) + own_sum.astype(jnp.float32)).astype(jnp.bfloat16)
            keep_final = active & (virt_idx == 1) & (stage_idx == stages - 1)
            old_out = lax.dynamic_index_in_dim(out_box, micro_idx, 0, keepdims=False)
            out_box = lax.dynamic_update_index_in_dim(out_box, jnp.where(keep_final, new_shard, old_out), micro_idx, 0)
            received = lax.ppermute(new_shard, "pp", next_perm)
            sent_idx = tick_idx - prev_stage
            store_it = (sent_idx >= 0) & (sent_idx <= last_work) & ((stage_idx != 0) | (sent_idx < micro_count))
            slot_idx = jnp.clip(sent_idx, 0, last_work) % micro_count
            old_in = lax.dynamic_index_in_dim(in_box, slot_idx, 0, keepdims=False)
            in_box = lax.dynamic_update_index_in_dim(in_box, jnp.where(store_it, received, old_in), slot_idx, 0)
            return in_box, out_box

        tick_count = 2 * micro_count + stages - 1
        _, out_box = lax.fori_loop(0, tick_count, run_tick, (x_loc, jnp.zeros_like(x_loc)))
        return lax.psum_scatter(out_box, "pp", scatter_dimension=0, tiled=True)

    return jax.shard_map(per_device, mesh=mesh, in_specs=(P("dp", "tp", None), P(None, "pp", None), P(None, "pp", None, "tp"), P(None, "pp", "tp", None)), out_specs=P(("dp", "pp"), "tp", None), check_vma=False)
```

profile of v0, /device:TPU:4, one launch (start us, length us, event | category | flops | bytes accessed | tf_op | source)
XLA Modules:
  0.0 6916.5 jit_solution(7072260837030266617)
XLA Ops:
  14.6 6841.7 %while.17 = (s32[]{:T(128)}, bf16[64,16,2048]{2,1,0:T(8,128)(2,1)}, bf16[64,16,2048]{2,1,0:T(8,128)(2,1)}, s32[]{:T(128)}, pred[]{:T(512)}, /*index=5*/s32[]{:T(...) while((s32[]{:T(128)}, bf16[64,16,2048]{2,1,0:T(8,128)(2,1)}, ...), condition=%wide.region_4.5_spmd, body=%wide.region_0.4_spmd.sunk | while | flops 1076824192 | bytes 20931000 | solution.py:58
  87.5 26.8 all-reduce.2.cloned.1.call-done
  193.6 26.8 all-reduce.2.cloned.1.call-done
  299.7 26.8 all-reduce.2.cloned.1.call-done
  405.8 26.8 all-reduce.2.cloned.1.call-done
  458.8 26.8 all-reduce.2.cloned.1.call-done
  511.8 26.8 all-reduce.2.cloned.1.call-done
  617.9 26.8 all-reduce.2.cloned.1.call-done
  670.9 26.8 all-reduce.2.cloned.1.call-done
  724.0 26.8 all-reduce.2.cloned.1.call-done
  777.0 26.8 all-reduce.2.cloned.1.call-done
  830.0 26.8 all-reduce.2.cloned.1.call-done
  883.1 26.8 all-reduce.2.cloned.1.call-done
  989.2 26.8 all-reduce.2.cloned.1.call-done
  1042.2 26.8 all-reduce.2.cloned.1.call-done
  1095.2 26.8 all-reduce.2.cloned.1.call-done
  1148.3 26.8 all-reduce.2.cloned.1.call-done
  1201.3 26.8 all-reduce.2.cloned.1.call-done
  1254.3 26.8 all-reduce.2.cloned.1.call-done
  1413.4 26.8 all-reduce.2.cloned.1.call-done
  1466.5 26.8 all-reduce.2.cloned.1.call-done
  1519.5 26.8 all-reduce.2.cloned.1.call-done
  1572.6 26.8 all-reduce.2.cloned.1.call-done
  1625.6 26.8 all-reduce.2.cloned.1.call-done
  1678.6 26.8 all-reduce.2.cloned.1.call-done
  1731.7 26.8 all-reduce.2.cloned.1.call-done
  1784.7 26.8 all-reduce.2.cloned.1.call-done
  1837.7 26.8 all-reduce.2.cloned.1.call-done
  1890.8 26.8 all-reduce.2.cloned.1.call-done
  1943.8 26.8 all-reduce.2.cloned.1.call-done
  2049.9 26.8 all-reduce.2.cloned.1.call-done
  2102.9 26.8 all-reduce.2.cloned.1.call-done
  2155.9 26.8 all-reduce.2.cloned.1.call-done
  2209.0 26.8 all-reduce.2.cloned.1.call-done
  2262.0 26.8 all-reduce.2.cloned.1.call-done
  2368.1 26.8 all-reduce.2.cloned.1.call-done
  2421.1 26.8 all-reduce.2.cloned.1.call-done
  2474.1 26.8 all-reduce.2.cloned.1.call-done
  2580.2 26.8 all-reduce.2.cloned.1.call-done
  2633.3 26.8 all-reduce.2.cloned.1.call-done
  2686.3 26.8 all-reduce.2.cloned.1.call-done
  2739.3 26.8 all-reduce.2.cloned.1.call-done
  2792.3 26.8 all-reduce.2.cloned.1.call-done
  2898.4 26.8 all-reduce.2.cloned.1.call-done
  2951.4 26.8 all-reduce.2.cloned.1.call-done
  3004.5 26.8 all-reduce.2.cloned.1.call-done
  3057.5 26.8 all-reduce.2.cloned.1.call-done
  3110.5 26.8 all-reduce.2.cloned.1.call-done
  3163.6 26.8 all-reduce.2.cloned.1.call-done
  3269.6 26.8 all-reduce.2.cloned.1.call-done
  3322.7 26.8 all-reduce.2.cloned.1.call-done
  3428.8 26.8 all-reduce.2.cloned.1.call-done
  3694.0 26.8 all-reduce.2.cloned.1.call-done
  3800.0 26.8 all-reduce.2.cloned.1.call-done
  4065.2 26.8 all-reduce.2.cloned.1.call-done
  4436.5 26.8 all-reduce.2.cloned.1.call-done
  4860.8 26.8 all-reduce.2.cloned.1.call-done
  5072.9 26.8 all-reduce.2.cloned.1.call-done
  5815.4 26.8 all-reduce.2.cloned.1.call-done
  6080.6 26.8 all-reduce.2.cloned.1.call-done
  6398.7 26.8 all-reduce.2.cloned.1.call-done
  6451.8 26.8 all-reduce.2.cloned.1.call-done
  6557.8 26.8 all-reduce.2.cloned.1.call-done
  6856.8 52.5 reduce-scatter.2.cloned.1.call-done
  (2008 shorter events, 5181.6 us)
Async XLA Ops:
  14.6 46.7 all-reduce.2.cloned.1.call-start
  67.7 46.6 all-reduce.2.cloned.1.call-start
  120.7 46.6 all-reduce.2.cloned.1.call-start
  226.8 46.6 all-reduce.2.cloned.1.call-start
  279.8 46.6 all-reduce.2.cloned.1.call-start
  332.9 46.6 all-reduce.2.cloned.1.call-start
  438.9 46.6 all-reduce.2.cloned.1.call-start
  545.0 46.6 all-reduce.2.cloned.1.call-start
  704.1 46.6 all-reduce.2.cloned.1.call-start
  757.2 46.6 all-reduce.2.cloned.1.call-start
  863.2 46.6 all-reduce.2.cloned.1.call-start
  916.3 46.6 all-reduce.2.cloned.1.call-start
  969.3 46.6 all-reduce.2.cloned.1.call-start
  1022.3 46.6 all-reduce.2.cloned.1.call-start
  1128.4 46.6 all-reduce.2.cloned.1.call-start
  1287.5 46.6 all-reduce.2.cloned.1.call-start
  1446.6 46.6 all-reduce.2.cloned.1.call-start
  1499.7 46.6 all-reduce.2.cloned.1.call-start
  1764.8 46.6 all-reduce.2.cloned.1.call-start
  1870.9 46.6 all-reduce.2.cloned.1.call-start
  1923.9 46.6 all-reduce.2.cloned.1.call-start
  1977.0 46.6 all-reduce.2.cloned.1.call-start
  2083.0 46.6 all-reduce.2.cloned.1.call-start
  2136.1 46.6 all-reduce.2.cloned.1.call-start
  2242.1 46.6 all-reduce.2.cloned.1.call-start
  2295.2 46.6 all-reduce.2.cloned.1.call-start
  2348.2 46.6 all-reduce.2.cloned.1.call-start
  2507.3 46.6 all-reduce.2.cloned.1.call-start
  2984.6 46.6 all-reduce.2.cloned.1.call-start
  3090.7 46.6 all-reduce.2.cloned.1.call-start
  3302.8 46.6 all-reduce.2.cloned.1.call-start
  3355.9 46.6 all-reduce.2.cloned.1.call-start
  3408.9 46.6 all-reduce.2.cloned.1.call-start
  3462.0 46.6 all-reduce.2.cloned.1.call-start
  3515.0 46.6 all-reduce.2.cloned.1.call-start
  3674.1 46.6 all-reduce.2.cloned.1.call-start
  3727.1 46.6 all-reduce.2.cloned.1.call-start
  3833.2 46.6 all-reduce.2.cloned.1.call-start
  4098.4 46.6 all-reduce.2.cloned.1.call-start
  4151.4 46.6 all-reduce.2.cloned.1.call-start
  4257.5 46.6 all-reduce.2.cloned.1.call-start
  4310.6 46.6 all-reduce.2.cloned.1.call-start
  4363.6 46.6 all-reduce.2.cloned.1.call-start
  4416.6 46.6 all-reduce.2.cloned.1.call-start
  4522.7 46.6 all-reduce.2.cloned.1.call-start
  4681.8 46.6 all-reduce.2.cloned.1.call-start
  4840.9 46.6 all-reduce.2.cloned.1.call-start
  4893.9 46.6 all-reduce.2.cloned.1.call-start
  5159.1 46.6 all-reduce.2.cloned.1.call-start
  5265.2 46.6 all-reduce.2.cloned.1.call-start
  5318.2 46.6 all-reduce.2.cloned.1.call-start
  5371.2 46.6 all-reduce.2.cloned.1.call-start
  5477.3 46.6 all-reduce.2.cloned.1.call-start
  5530.3 46.6 all-reduce.2.cloned.1.call-start
  5636.4 46.6 all-reduce.2.cloned.1.call-start
  5689.4 46.6 all-reduce.2.cloned.1.call-start
  5742.5 46.6 all-reduce.2.cloned.1.call-start
  5901.6 46.6 all-reduce.2.cloned.1.call-start
  6378.9 46.6 all-reduce.2.cloned.1.call-start
  6485.0 46.6 all-reduce.2.cloned.1.call-start
  6697.1 46.6 all-reduce.2.cloned.1.call-start
  6750.1 46.6 all-reduce.2.cloned.1.call-start
  6803.2 46.7 all-reduce.2.cloned.1.call-start
  6856.3 53.1 reduce-scatter.2.cloned.1.call-start
  (196 other events, 3631.4 us)
Sparse Core Ops, SparseCore 0:
  86.8 27.4 all-reduce.1
  192.9 27.4 all-reduce.1
  298.9 27.4 all-reduce.1
  405.0 27.4 all-reduce.1
  458.0 27.4 all-reduce.1
  511.1 27.4 all-reduce.1
  617.2 27.4 all-reduce.1
  670.2 27.4 all-reduce.1
  723.2 27.4 all-reduce.1
  776.3 27.4 all-reduce.1
  829.3 27.4 all-reduce.1
  882.3 27.4 all-reduce.1
  988.4 27.4 all-reduce.1
  1041.4 27.4 all-reduce.1
  1094.5 27.4 all-reduce.1
  1147.5 27.4 all-reduce.1
  1200.6 27.4 all-reduce.1
  1253.6 27.4 all-reduce.1
  1412.7 27.4 all-reduce.1
  1465.7 27.4 all-reduce.1
  1518.8 27.4 all-reduce.1
  1571.8 27.4 all-reduce.1
  1624.8 27.4 all-reduce.1
  1677.9 27.4 all-reduce.1
  1730.9 27.4 all-reduce.1
  1783.9 27.4 all-reduce.1
  1837.0 27.4 all-reduce.1
  1890.0 27.4 all-reduce.1
  1943.0 27.4 all-reduce.1
  2049.1 27.4 all-reduce.1
  2102.1 27.4 all-reduce.1
  2155.2 27.4 all-reduce.1
  2208.2 27.4 all-reduce.1
  2261.2 27.4 all-reduce.1
  2367.3 27.4 all-reduce.1
  2420.4 27.4 all-reduce.1
  2473.4 27.4 all-reduce.1
  2579.5 27.4 all-reduce.1
  2632.5 27.4 all-reduce.1
  2685.5 27.4 all-reduce.1
  2738.6 27.4 all-reduce.1
  2791.6 27.4 all-reduce.1
  2897.7 27.4 all-reduce.1
  2950.7 27.4 all-reduce.1
  3003.7 27.4 all-reduce.1
  3056.8 27.4 all-reduce.1
  3109.8 27.4 all-reduce.1
  3162.8 27.4 all-reduce.1
  3268.9 27.4 all-reduce.1
  3321.9 27.4 all-reduce.1
  3428.0 27.4 all-reduce.1
  3587.1 27.4 all-reduce.1
  3693.2 27.4 all-reduce.1
  3799.3 27.4 all-reduce.1
  3852.3 27.4 all-reduce.1
  3905.4 27.4 all-reduce.1
  4011.4 27.4 all-reduce.1
  4064.5 27.4 all-reduce.1
  4117.5 27.4 all-reduce.1
  4170.5 27.4 all-reduce.1
  4223.6 27.4 all-reduce.1
  4276.6 27.4 all-reduce.1
  4435.7 27.4 all-reduce.1
  4860.0 27.4 all-reduce.1
  (65 shorter events, 1783.2 us)
Sparse Core Ops, SparseCore 1:
  6859.0 50.3 reduce-scatter.1
where the time goes:
time: 6940 us; the launch traced here: 6920 us
  waiting for transfers between devices  3990 us (57%)
  matrix products  1240 us (18%)
  blocking collectives  1040 us (15%)
  other arithmetic  326 us (5%)
  local copies, waits for them, and re-layouts  231 us (3%)
  starting transfers between devices  72.7 us (1%)
    psum x129, waiting for transfers between devices, run_tick(): reduced = lax.psum(part_prod, 'tp')  3460 us
    dot_general x129, matrix products, run_tick(): jnp.dot(hidden, w_second, preferred_element_type=jnp.float32)  1240 us
    all_gather x129, blocking collectives, run_tick(): cur_full = lax.all_gather(cur_shard, 'tp', axis=0, tiled=True)  1040 us
    ppermute x129, waiting for transfers between devices, run_tick(): received = lax.ppermute(new_shard, 'pp', next_perm)  478 us
    dynamic_update_slice x129, other arithmetic, run_tick(): lax.dynamic_update_index_in_dim(out_box, jnp.where(keep_final, new_shard,...  192 us
  transfers between devices with their start and end apart: 259, of which 259 were waited for; matrix products, arithmetic and copies ran while one was open for 2% of the time, Pallas kernels for 0%

commit v1 on v0

v1 whole, which is shorter than its diff:
```python
import functools

import jax
import jax.numpy as jnp
from jax import lax
from jax.experimental import pallas as pl
from jax.experimental.pallas import tpu as pltpu
from jax.sharding import PartitionSpec as P

NORM_EPS = 1e-5
MESH = pl.DeviceIdType.MESH

MICRO_PER_ITEM = 2
LOOKAHEAD = 3
LAG_FINAL = 3
COL_BLOCK = 512


def mlp_kernel(dims, x_ref, gain_ref, w1_hbm, w2_hbm, out_ref,
               w1, w2, inbox, hbuf, abuf, qbuf, pair_in, sum_out, sum_in,
               w_sem, agx_s, agx_r, agd_s, agd_r, rsd_s, rsd_r, rsx_s, rsx_r, y_s, y_r, out_r):
    items, rows, width, ring = dims
    work = 2 * items
    hid = w1.shape[2]
    stage = lax.axis_index("pp")
    rank = lax.axis_index("tp")
    cx, cc = rank // 2, rank % 2
    sibling = {"tp": 2 * cx + (1 - cc)}
    across = {"tp": 2 * (1 - cx) + cc}
    other_stage = {"pp": 1 - stage}

    @pl.when(stage == 0)
    def _():
        @pl.loop(0, items)
        def _(i):
            pltpu.make_async_copy(x_ref.at[i], inbox.at[i], y_r.at[i]).start()

    w_copies = []
    for v in range(2):
        w_copies.append((pltpu.make_async_copy(w1_hbm.at[v], w1.at[v], w_sem.at[2 * v]),
                         pltpu.make_async_copy(w2_hbm.at[v], w2.at[v], w_sem.at[2 * v + 1])))
    for pair in w_copies:
        for cp in pair:
            cp.start()

    barrier = pltpu.get_barrier_semaphore()
    for dev in (sibling, across, other_stage):
        pl.semaphore_signal(barrier, inc=1, device_id=dev, device_id_type=MESH)
    pl.semaphore_wait(barrier, 3)

    def remote(src, dst, s_sem, r_sem, dev):
        return pltpu.make_async_remote_copy(src_ref=src, dst_ref=dst, send_sem=s_sem, recv_sem=r_sem,
                                            device_id=dev, device_id_type=MESH)

    def copy_agx(slot, src_x):
        ref = hbuf.at[slot, cc, src_x]
        return remote(ref, ref, agx_s.at[slot], agx_r.at[slot], across)

    def copy_agd(slot, src_c):
        ref = hbuf.at[slot, src_c]
        return remote(ref, ref, agd_s.at[slot], agd_r.at[slot], sibling)

    def copy_rsd(slot):
        return remote(qbuf.at[slot, 1 - cc], pair_in.at[slot], rsd_s.at[slot], rsd_r.at[slot], sibling)

    def copy_rsx(slot):
        return remote(sum_out.at[slot], sum_in.at[slot], rsx_s.at[slot], rsx_r.at[slot], across)

    def norm_and_send(w):
        slot = lax.rem(w, ring)
        v = w // items
        pltpu.make_async_copy(inbox.at[w], inbox.at[w], y_r.at[w]).wait()
        y = inbox[w].astype(jnp.float32)
        mean = jnp.mean(y, axis=-1, keepdims=True)
        cen = y - mean
        var = jnp.mean(cen * cen, axis=-1, keepdims=True)
        gain = gain_ref[v].astype(jnp.float32)
        hbuf[slot, cc, cx] = (cen * lax.rsqrt(var + NORM_EPS) * gain).astype(jnp.bfloat16)
        copy_agx(slot, cx).start()

    def forward(w):
        slot = lax.rem(w, ring)
        copy_agx(slot, 1 - cx).wait_recv()
        copy_agd(slot, cc).start()

    def first_matmul(w):
        slot = lax.rem(w, ring)
        v = w // items
        copy_agd(slot, 1 - cc).wait_recv()
        for n in range(0, hid, COL_BLOCK):
            h = hbuf[slot].reshape(4 * rows, width)
            z = jnp.dot(h, w1[v, :, n:n + COL_BLOCK], preferred_element_type=jnp.float32)
            abuf[:, n:n + COL_BLOCK] = jax.nn.gelu(z).astype(jnp.bfloat16)
        copy_agx(slot, cx).wait_send()
        copy_agd(slot, cc).wait_send()

    def second_matmul(w):
        slot = lax.rem(w, ring)
        v = w // items
        for n in range(0, width, COL_BLOCK):
            q = jnp.dot(abuf[...], w2[v, :, n:n + COL_BLOCK], preferred_element_type=jnp.float32)
            qbuf[slot, :, :, :, n:n + COL_BLOCK] = q.astype(jnp.bfloat16).reshape(2, 2, rows, COL_BLOCK)
        copy_rsd(slot).start()

    def relay(w):
        slot = lax.rem(w, ring)
        cp = copy_rsd(slot)
        cp.wait_send()
        cp.wait_recv()
        total = qbuf[slot, cc, 1 - cx].astype(jnp.float32) + pair_in[slot, 1 - cx].astype(jnp.float32)
        sum_out[slot] = total.astype(jnp.bfloat16)
        copy_rsx(slot).start()

    def y_send_wait(k):
        pltpu.make_async_copy(inbox.at[0], inbox.at[0], y_s.at[k]).wait()

    def finish(w):
        slot = lax.rem(w, ring)
        v = w // items
        i = lax.rem(w, items)
        cp = copy_rsx(slot)
        cp.wait_send()
        cp.wait_recv()
        ysem = y_s.at[lax.rem(w, 2)]

        @pl.when(w >= 2)
        def _():
            y_send_wait(lax.rem(w, 2))

        total = qbuf[slot, cc, cx].astype(jnp.float32) + pair_in[slot, cx].astype(jnp.float32)
        total = total + sum_in[slot].astype(jnp.float32)
        inbox[w] = (inbox[w].astype(jnp.float32) + total).astype(jnp.bfloat16)
        last = (stage == 1) & (v == 1)
        half = items // 2

        @pl.when(jnp.logical_not(last))
        def _():
            dst = w + stage * items
            remote(inbox.at[w], inbox.at[dst], ysem, y_r.at[dst], other_stage).start()

        @pl.when(last & (i < half))
        def _():
            remote(inbox.at[w], out_ref.at[i], ysem, out_r.at[0], other_stage).start()

        @pl.when(last & (i >= half))
        def _():
            pltpu.make_async_copy(inbox.at[w], out_ref.at[i - half], ysem).start()

    for w in range(LOOKAHEAD):
        norm_and_send(w)
    forward(0)

    def tick(t, carry):
        @pl.when(t + 1 < work)
        def _():
            forward(t + 1)

        for v in range(2):
            @pl.when(t == v * items)
            def _():
                for cp in w_copies[v]:
                    cp.wait()

        @pl.when(t < work)
        def _():
            first_matmul(t)

        @pl.when((t >= 1) & (t <= work))
        def _():
            relay(t - 1)

        @pl.when(t >= LAG_FINAL)
        def _():
            finish(t - LAG_FINAL)

        @pl.when(t + LOOKAHEAD < work)
        def _():
            norm_and_send(t + LOOKAHEAD)

        @pl.when(t < work)
        def _():
            second_matmul(t)

        return carry

    lax.fori_loop(0, work + LAG_FINAL, tick, 0)
    for k in range(2):
        y_send_wait(k)

    @pl.when(stage == 0)
    def _():
        pltpu.make_async_copy(out_ref, out_ref, out_r.at[0]).wait()


def solution(mesh):
    def per_device(x_loc, gain_loc, w_in_loc, w_out_loc):
        micro, toks, width = x_loc.shape
        items = micro // MICRO_PER_ITEM
        rows = MICRO_PER_ITEM * toks
        hid = w_in_loc.shape[3]
        ring = LOOKAHEAD + LAG_FINAL
        bf16 = jnp.bfloat16
        dma = pltpu.SemaphoreType.DMA
        any_spec = pl.BlockSpec(memory_space=pl.ANY)
        flops = 2 * 2 * micro * 4 * toks * width * hid * 2
        out = pl.pallas_call(
            functools.partial(mlp_kernel, (items, rows, width, ring)),
            out_shape=jax.ShapeDtypeStruct((items // 2, rows, width), bf16),
            in_specs=[any_spec, pl.BlockSpec(memory_space=pltpu.VMEM), any_spec, any_spec],
            out_specs=any_spec,
            scratch_shapes=[
                pltpu.VMEM((2, width, hid), bf16),
                pltpu.VMEM((2, hid, width), bf16),
                pltpu.VMEM((2 * items, rows, width), bf16),
                pltpu.VMEM((ring, 2, 2, rows, width), bf16),
                pltpu.VMEM((4 * rows, hid), bf16),
                pltpu.VMEM((ring, 2, 2, rows, width), bf16),
                pltpu.VMEM((ring, 2, rows, width), bf16),
                pltpu.VMEM((ring, rows, width), bf16),
                pltpu.VMEM((ring, rows, width), bf16),
                dma((4,)),
            ] + [dma((ring,))] * 8 + [dma((2,)), dma((2 * items,)), dma((1,))],
            compiler_params=pltpu.CompilerParams(collective_id=0, has_side_effects=True,
                                                 vmem_limit_bytes=67043328),
            cost_estimate=pl.CostEstimate(flops=flops, bytes_accessed=2 ** 26, transcendentals=0),
        )(x_loc.reshape(items, rows, width), gain_loc, w_in_loc[:, 0], w_out_loc[:, 0])
        return out.reshape(micro // 2, toks, width)

    return jax.shard_map(per_device, mesh=mesh, in_specs=(P("dp", "tp", None), P(None, "pp", None), P(None, "pp", None, "tp"), P(None, "pp", "tp", None)), out_specs=P(("dp", "pp"), "tp", None), check_vma=False)
```

time: 6940 us -> 407 us (0.06)
  waiting for transfers between devices: 3990 us -> 0 us
  matrix products: 1240 us -> 0 us
  blocking collectives: 1040 us -> 0 us
  Pallas kernels: 0 us -> 402 us
  other arithmetic: 326 us -> 0 us
  local copies, waits for them, and re-layouts: 231 us -> 4.47 us
  starting transfers between devices: 72.7 us -> 0 us
    psum x129 -> x0, waiting for transfers between devices: 3460 us -> none  [run_tick(): reduced = lax.psum(part_prod, 'tp')]
    dot_general x129 -> x0, matrix products: 1240 us -> none  [run_tick(): jnp.dot(hidden, w_second, preferred_element_type=jnp.float32)]
    all_gather x129 -> x0, blocking collectives: 1040 us -> none  [run_tick(): cur_full = lax.all_gather(cur_shard, 'tp', axis=0, tiled=True)]
    ppermute x129 -> x0, waiting for transfers between devices: 478 us -> none  [run_tick(): received = lax.ppermute(new_shard, 'pp', next_perm)]
    pallas_call x0 -> x1, Pallas kernels: none -> 402 us  [per_device(): pl.pallas_call(functools.partial(mlp_kernel, (items, rows, width, ring)),...]
    dynamic_update_slice x258 -> x0, other arithmetic: 274 us -> none  [the longest x129 192 us: run_tick(): lax.dynamic_update_index_in_dim(out_box, jnp.where(keep_final, new_shard,...]
    dynamic_slice x258 -> x0, local copies, waits for them, and re-layouts: 224 us -> none  [the longest x129 114 us: run_tick(): old_in = lax.dynamic_index_in_dim(in_box, slot_idx, 0, keepdims=False)]
    ppermute x129 -> x0, starting transfers between devices: 72.4 us -> none  [run_tick(): received = lax.ppermute(new_shard, 'pp', next_perm)]
  transfers between devices with their start and end apart: 259 -> 0, of which waited for: 259 -> 0; matrix products, arithmetic and copies ran while one was open for 2% -> 0% of each run, Pallas kernels for 0% -> 0%
where the time goes in v1:
time: 407 us
  Pallas kernels  402 us (99%)
  local copies, waits for them, and re-layouts  4.47 us (1%)
    pallas_call x1, Pallas kernels, per_device(): pl.pallas_call(functools.partial(mlp_kernel, (items, rows, width, ring)),...  402 us

profile of v1, /device:TPU:4, one launch (start us, length us, event | category | flops | bytes accessed | tf_op | source)
XLA Modules:
  0.0 406.7 jit_solution(3609967268531954240)
XLA Ops:
  0.0 1.3 copy.5.gain_ref
  1.3 402.2 %shard_map.46 = bf16[16,32,2048]{2,1,0:T(8,128)(2,1)} custom-call(bf16[32,32,2048]{2,1,0:T(8,128)(2,1)} %bitcast.7, bf16[2,1,2048]{2,1,0:T(2,128)(2,1)} %copy.5.gain_ref, bf16[2,2048,2048]{2,1,0:T(8,128)(2,1)} %bitcast.5, bf16[2,2048,2048]{2,1,0:T(8,128)(2,1)} %bitcast.6), custom_call_target="tpu_custom_call" | custom-call | flops 137438953472 | bytes 67108864 | tf_op jit(solution)/shard_map/pallas_call | solution.py:206
  403.5 3.2 copy.7

commit v2 on v1

--- a/solution.py
+++ b/solution.py
@@ -11,14 +11,19 @@
 MESH = pl.DeviceIdType.MESH
 
 MICRO_PER_ITEM = 2
-LOOKAHEAD = 3
+LOOKAHEAD = 4
 LAG_FINAL = 3
 COL_BLOCK = 512
+HEAD_FAR = 16
+HEAD_SKIP = 3
+MID_DIAG = 2
+MID_FIRST = 36
+LAST_DIAG = 2
 
 
 def mlp_kernel(dims, x_ref, gain_ref, w1_hbm, w2_hbm, out_ref,
-               w1, w2, inbox, hbuf, abuf, qbuf, pair_in, sum_out, sum_in,
-               w_sem, agx_s, agx_r, agd_s, agd_r, rsd_s, rsd_r, rsx_s, rsx_r, y_s, y_r, out_r):
+               w1, w2, inbox, hbuf, abuf, qbuf, pair_in, sum_out, sum_in, far,
+               w_sem, agx_s, agx_r, agd_s, agd_r, rsd_s, rsd_r, rsx_s, rsx_r, y_s, y_r, out_r, far_s, far_r):
     items, rows, width, ring = dims
     work = 2 * items
     hid = w1.shape[2]
@@ -28,6 +33,23 @@
     sibling = {"tp": 2 * cx + (1 - cc)}
     across = {"tp": 2 * (1 - cx) + cc}
     other_stage = {"pp": 1 - stage}
+    diagonal = {"pp": 1 - stage, "tp": 2 * (1 - cx) + cc}
+
+    def early_far(w):
+        return (w < HEAD_FAR) & (lax.rem(w, HEAD_SKIP) != HEAD_SKIP - 1)
+
+    def mid_far(w):
+        return (w >= MID_FIRST) & (w < MID_FIRST + MID_DIAG)
+
+    def last_far(w):
+        return w >= work - LAST_DIAG
+
+    def is_far(w):
+        return ((stage == 0) & early_far(w)) | ((stage == 1) & (mid_far(w) | last_far(w)))
+
+    def far_slot(w):
+        late = jnp.where(w >= work - LAST_DIAG, w - (work - LAST_DIAG) + MID_DIAG, w - MID_FIRST)
+        return jnp.where(w < HEAD_FAR, w, HEAD_FAR + late)
 
     @pl.when(stage == 0)
     def _():
@@ -39,14 +61,13 @@
     for v in range(2):
         w_copies.append((pltpu.make_async_copy(w1_hbm.at[v], w1.at[v], w_sem.at[2 * v]),
                          pltpu.make_async_copy(w2_hbm.at[v], w2.at[v], w_sem.at[2 * v + 1])))
-    for pair in w_copies:
-        for cp in pair:
-            cp.start()
+    for cp in w_copies[0]:
+        cp.start()
 
     barrier = pltpu.get_barrier_semaphore()
-    for dev in (sibling, across, other_stage):
+    for dev in (sibling, across, other_stage, diagonal):
         pl.semaphore_signal(barrier, inc=1, device_id=dev, device_id_type=MESH)
-    pl.semaphore_wait(barrier, 3)
+    pl.semaphore_wait(barrier, 4)
 
     def remote(src, dst, s_sem, r_sem, dev):
         return pltpu.make_async_remote_copy(src_ref=src, dst_ref=dst, send_sem=s_sem, recv_sem=r_sem,
@@ -66,21 +87,56 @@
     def copy_rsx(slot):
         return remote(sum_out.at[slot], sum_in.at[slot], rsx_s.at[slot], rsx_r.at[slot], across)
 
-    def norm_and_send(w):
-        slot = lax.rem(w, ring)
-        v = w // items
-        pltpu.make_async_copy(inbox.at[w], inbox.at[w], y_r.at[w]).wait()
-        y = inbox[w].astype(jnp.float32)
+    def copy_far(src, k):
+        return remote(src, far.at[k], far_s.at[k], far_r.at[k], diagonal)
+
+    def head_far(k, start):
+        own = k == 0
+
+        @pl.when((stage == 0) & own)
+        def _():
+            cp = remote(x_ref.at[k], far.at[k], far_s.at[k], far_r.at[k], across)
+            cp.start() if start else cp.wait_send()
+
+        @pl.when((stage == 1) & jnp.logical_not(own) & early_far(k))
+        def _():
+            cp = copy_far(x_ref.at[k], k)
+            cp.start() if start else cp.wait_send()
+
+    @pl.loop(0, HEAD_FAR)
+    def _(k):
+        head_far(k, True)
+
+    def normed(resid, v):
+        y = resid.astype(jnp.float32)
         mean = jnp.mean(y, axis=-1, keepdims=True)
         cen = y - mean
         var = jnp.mean(cen * cen, axis=-1, keepdims=True)
         gain = gain_ref[v].astype(jnp.float32)
-        hbuf[slot, cc, cx] = (cen * lax.rsqrt(var + NORM_EPS) * gain).astype(jnp.bfloat16)
-        copy_agx(slot, cx).start()
+        return (cen * lax.rsqrt(var + NORM_EPS) * gain).astype(jnp.bfloat16)
+
+    def norm_and_send(w):
+        slot = lax.rem(w, ring)
+        pltpu.make_async_copy(inbox.at[w], inbox.at[w], y_r.at[w]).wait()
+        hbuf[slot, cc, cx] = normed(inbox[w], w // items)
+
+        @pl.when(jnp.logical_not(is_far(w)))
+        def _():
+            copy_agx(slot, cx).start()
 
     def forward(w):
         slot = lax.rem(w, ring)
-        copy_agx(slot, 1 - cx).wait_recv()
+
+        @pl.when(jnp.logical_not(is_far(w)))
+        def _():
+            copy_agx(slot, 1 - cx).wait_recv()
+
+        @pl.when(is_far(w))
+        def _():
+            k = far_slot(w)
+            pltpu.make_async_copy(far.at[k], far.at[k], far_r.at[k]).wait()
+            hbuf[slot, cc, 1 - cx] = normed(far[k], w // items)
+
         copy_agd(slot, cc).start()
 
     def first_matmul(w):
@@ -91,7 +147,11 @@
             h = hbuf[slot].reshape(4 * rows, width)
             z = jnp.dot(h, w1[v, :, n:n + COL_BLOCK], preferred_element_type=jnp.float32)
             abuf[:, n:n + COL_BLOCK] = jax.nn.gelu(z).astype(jnp.bfloat16)
-        copy_agx(slot, cx).wait_send()
+
+        @pl.when(jnp.logical_not(is_far(w)))
+        def _():
+            copy_agx(slot, cx).wait_send()
+
         copy_agd(slot, cc).wait_send()
 
     def second_matmul(w):
@@ -138,6 +198,10 @@
             dst = w + stage * items
             remote(inbox.at[w], inbox.at[dst], ysem, y_r.at[dst], other_stage).start()
 
+        @pl.when((stage == 0) & (mid_far(w) | last_far(w)))
+        def _():
+            copy_far(inbox.at[w], far_slot(w)).start()
+
         @pl.when(last & (i < half))
         def _():
             remote(inbox.at[w], out_ref.at[i], ysem, out_r.at[0], other_stage).start()
@@ -154,6 +218,11 @@
         @pl.when(t + 1 < work)
         def _():
             forward(t + 1)
+
+        @pl.when(t == 1)
+        def _():
+            for cp in w_copies[1]:
+                cp.start()
 
         for v in range(2):
             @pl.when(t == v * items)
@@ -186,6 +255,15 @@
     lax.fori_loop(0, work + LAG_FINAL, tick, 0)
     for k in range(2):
         y_send_wait(k)
+
+    @pl.loop(0, HEAD_FAR)
+    def _(k):
+        head_far(k, False)
+
+    @pl.when(stage == 0)
+    def _():
+        for k in range(HEAD_FAR, HEAD_FAR + MID_DIAG + LAST_DIAG):
+            pltpu.make_async_copy(far.at[k], far.at[k], far_s.at[k]).wait()
 
     @pl.when(stage == 0)
     def _():
@@ -218,8 +296,10 @@
                 pltpu.VMEM((ring, 2, rows, width), bf16),
                 pltpu.VMEM((ring, rows, width), bf16),
                 pltpu.VMEM((ring, rows, width), bf16),
+                pltpu.VMEM((HEAD_FAR + MID_DIAG + LAST_DIAG, rows, width), bf16),
                 dma((4,)),
-            ] + [dma((ring,))] * 8 + [dma((2,)), dma((2 * items,)), dma((1,))],
+            ] + [dma((ring,))] * 8 + [dma((2,)), dma((2 * items,)), dma((1,))]
+            + [dma((HEAD_FAR + MID_DIAG + LAST_DIAG,))] * 2,
             compiler_params=pltpu.CompilerParams(collective_id=0, has_side_effects=True,
                                                  vmem_limit_bytes=67043328),
             cost_estimate=pl.CostEstimate(flops=flops, bytes_accessed=2 ** 26, transcendentals=0),

time: 407 us -> 388 us (0.953)
  Pallas kernels: 402 us -> 383 us
    pallas_call x1, Pallas kernels: 402 us -> 383 us  [per_device(): pl.pallas_call(functools.partial(mlp_kernel, (items, rows, width, ring)),...]
where the time goes in v2:
time: 388 us
  Pallas kernels  383 us (99%)
  local copies, waits for them, and re-layouts  4.47 us (1%)
    pallas_call x1, Pallas kernels, per_device(): pl.pallas_call(functools.partial(mlp_kernel, (items, rows, width, ring)),...  383 us

profile of v2, /device:TPU:4, one launch (start us, length us, event | category | flops | bytes accessed | tf_op | source)
XLA Modules:
  0.0 387.5 jit_solution(4906432933414031438)
XLA Ops:
  0.0 1.3 copy.5.gain_ref
  1.3 383.0 %shard_map.46 = bf16[16,32,2048]{2,1,0:T(8,128)(2,1)} custom-call(bf16[32,32,2048]{2,1,0:T(8,128)(2,1)} %bitcast.7, bf16[2,1,2048]{2,1,0:T(2,128)(2,1)} %copy.5.gain_ref, bf16[2,2048,2048]{2,1,0:T(8,128)(2,1)} %bitcast.5, bf16[2,2048,2048]{2,1,0:T(8,128)(2,1)} %bitcast.6), custom_call_target="tpu_custom_call" | custom-call | flops 137438953472 | bytes 67108864 | tf_op jit(solution)/shard_map/pallas_call | solution.py:284
  384.3 3.2 copy.7

commit v3 on v2

--- a/solution.py
+++ b/solution.py
@@ -14,18 +14,22 @@
 LOOKAHEAD = 4
 LAG_FINAL = 3
 COL_BLOCK = 512
-HEAD_FAR = 16
-HEAD_SKIP = 3
-MID_DIAG = 2
-MID_FIRST = 36
+HEAD_FROM = 4
+HEAD_FAR = 20
+HEAD_STEP = 3
+HEAD_KEEP = 1
+MID_DIAG = 3
+MID_FIRST = 47
+MID_STEP = 4
 LAST_DIAG = 2
 
 
-def mlp_kernel(dims, x_ref, gain_ref, w1_hbm, w2_hbm, out_ref,
-               w1, w2, inbox, hbuf, abuf, qbuf, pair_in, sum_out, sum_in, far,
-               w_sem, agx_s, agx_r, agd_s, agd_r, rsd_s, rsd_r, rsx_s, rsx_r, y_s, y_r, out_r, far_s, far_r):
+def mlp_kernel(dims, x_ref, gain_hbm, w1_hbm, w2_hbm, out_ref,
+               gains, w1, w2, inbox, hbuf, abuf, qbuf, pair_in, sum_out, sum_in, far,
+               w_sem, agx_s, agx_r, agd_s, agd_r, rsd_s, rsd_r, rsx_s, rsx_r, y_s, y_r, out_r, far_s, far_r, g_sem):
     items, rows, width, ring = dims
     work = 2 * items
+    half = items // 2
     hid = w1.shape[2]
     stage = lax.axis_index("pp")
     rank = lax.axis_index("tp")
@@ -36,10 +40,11 @@
     diagonal = {"pp": 1 - stage, "tp": 2 * (1 - cx) + cc}
 
     def early_far(w):
-        return (w < HEAD_FAR) & (lax.rem(w, HEAD_SKIP) != HEAD_SKIP - 1)
+        return (w == 0) | ((w >= HEAD_FROM) & (w < HEAD_FAR) & (lax.rem(w, HEAD_STEP) != HEAD_KEEP))
 
     def mid_far(w):
-        return (w >= MID_FIRST) & (w < MID_FIRST + MID_DIAG)
+        past = w - MID_FIRST
+        return (past >= 0) & (past < MID_DIAG * MID_STEP) & (lax.rem(w, MID_STEP) == MID_FIRST % MID_STEP)
 
     def last_far(w):
         return w >= work - LAST_DIAG
@@ -48,8 +53,11 @@
         return ((stage == 0) & early_far(w)) | ((stage == 1) & (mid_far(w) | last_far(w)))
 
     def far_slot(w):
-        late = jnp.where(w >= work - LAST_DIAG, w - (work - LAST_DIAG) + MID_DIAG, w - MID_FIRST)
+        late = jnp.where(w >= work - LAST_DIAG, w - (work - LAST_DIAG) + MID_DIAG, (w - MID_FIRST) // MID_STEP)
         return jnp.where(w < HEAD_FAR, w, HEAD_FAR + late)
+
+    gain_copy = pltpu.make_async_copy(gain_hbm, gains, g_sem.at[0])
+    gain_copy.start()
 
     @pl.when(stage == 0)
     def _():
@@ -112,7 +120,8 @@
         mean = jnp.mean(y, axis=-1, keepdims=True)
         cen = y - mean
         var = jnp.mean(cen * cen, axis=-1, keepdims=True)
-        gain = gain_ref[v].astype(jnp.float32)
+        pair = gains[...].astype(jnp.float32)
+        gain = jnp.where(v == 0, pair[0:1], pair[1:2])
         return (cen * lax.rsqrt(var + NORM_EPS) * gain).astype(jnp.bfloat16)
 
     def norm_and_send(w):
@@ -183,15 +192,15 @@
         cp.wait_recv()
         ysem = y_s.at[lax.rem(w, 2)]
 
-        @pl.when(w >= 2)
+        @pl.when((w >= 2) & ((stage == 0) | (w - 2 < items + half)))
         def _():
             y_send_wait(lax.rem(w, 2))
 
         total = qbuf[slot, cc, cx].astype(jnp.float32) + pair_in[slot, cx].astype(jnp.float32)
         total = total + sum_in[slot].astype(jnp.float32)
-        inbox[w] = (inbox[w].astype(jnp.float32) + total).astype(jnp.bfloat16)
+        new = (inbox[w].astype(jnp.float32) + total).astype(jnp.bfloat16)
+        inbox[w] = new
         last = (stage == 1) & (v == 1)
-        half = items // 2
 
         @pl.when(jnp.logical_not(last))
         def _():
@@ -208,8 +217,9 @@
 
         @pl.when(last & (i >= half))
         def _():
-            pltpu.make_async_copy(inbox.at[w], out_ref.at[i - half], ysem).start()
-
+            out_ref[i - half] = new
+
+    gain_copy.wait()
     for w in range(LOOKAHEAD):
         norm_and_send(w)
     forward(0)
@@ -253,15 +263,14 @@
         return carry
 
     lax.fori_loop(0, work + LAG_FINAL, tick, 0)
-    for k in range(2):
-        y_send_wait(k)
-
     @pl.loop(0, HEAD_FAR)
     def _(k):
         head_far(k, False)
 
     @pl.when(stage == 0)
     def _():
+        for k in range(2):
+            y_send_wait(k)
         for k in range(HEAD_FAR, HEAD_FAR + MID_DIAG + LAST_DIAG):
             pltpu.make_async_copy(far.at[k], far.at[k], far_s.at[k]).wait()
 
@@ -283,10 +292,11 @@
         flops = 2 * 2 * micro * 4 * toks * width * hid * 2
         out = pl.pallas_call(
             functools.partial(mlp_kernel, (items, rows, width, ring)),
-            out_shape=jax.ShapeDtypeStruct((items // 2, rows, width), bf16),
-            in_specs=[any_spec, pl.BlockSpec(memory_space=pltpu.VMEM), any_spec, any_spec],
-            out_specs=any_spec,
+            out_shape=pltpu.VMEM((items // 2, rows, width), bf16),
+            in_specs=[any_spec] * 4,
+            out_specs=pl.BlockSpec(memory_space=pltpu.VMEM),
             scratch_shapes=[
+                pltpu.VMEM((2, width), bf16),
                 pltpu.VMEM((2, width, hid), bf16),
                 pltpu.VMEM((2, hid, width), bf16),
                 pltpu.VMEM((2 * items, rows, width), bf16),
@@ -299,11 +309,11 @@
                 pltpu.VMEM((HEAD_FAR + MID_DIAG + LAST_DIAG, rows, width), bf16),
                 dma((4,)),
             ] + [dma((ring,))] * 8 + [dma((2,)), dma((2 * items,)), dma((1,))]
-            + [dma((HEAD_FAR + MID_DIAG + LAST_DIAG,))] * 2,
+            + [dma((HEAD_FAR + MID_DIAG + LAST_DIAG,))] * 2 + [dma((1,))],
             compiler_params=pltpu.CompilerParams(collective_id=0, has_side_effects=True,
-                                                 vmem_limit_bytes=67043328),
+                                                 vmem_limit_bytes=60 * 2 ** 20),
             cost_estimate=pl.CostEstimate(flops=flops, bytes_accessed=2 ** 26, transcendentals=0),
-        )(x_loc.reshape(items, rows, width), gain_loc, w_in_loc[:, 0], w_out_loc[:, 0])
+        )(x_loc.reshape(items, rows, width), gain_loc[:, 0], w_in_loc[:, 0], w_out_loc[:, 0])
         return out.reshape(micro // 2, toks, width)
 
     return jax.shard_map(per_device, mesh=mesh, in_specs=(P("dp", "tp", None), P(None, "pp", None), P(None, "pp", None, "tp"), P(None, "pp", "tp", None)), out_specs=P(("dp", "pp"), "tp", None), check_vma=False)

time: 388 us -> 381 us (0.982)
  no operation moved by 1% of the time
where the time goes in v3:
time: 381 us
  Pallas kernels  380 us (100%)
    pallas_call x1, Pallas kernels, per_device(): pl.pallas_call(functools.partial(mlp_kernel, (items, rows, width, ring)),...  380 us

profile of v3, /device:TPU:4, one launch (start us, length us, event | category | flops | bytes accessed | tf_op | source)
XLA Modules:
  0.0 381.1 jit_solution(12194655556266890147)
XLA Ops:
  0.0 379.7 %shard_map.46 = bf16[16,32,2048]{2,1,0:T(8,128)(2,1)S(1)} custom-call(bf16[32,32,2048]{2,1,0:T(8,128)(2,1)} %bitcast.8, bf16[2,2048]{1,0:T(2,128)(2,1)} %bitcast.9, bf16[2,2048,2048]{2,1,0:T(8,128)(2,1)} %bitcast.6, bf16[2,2048,2048]{2,1,0:T(8,128)(2,1)} %bitcast.7), custom_call_target="tpu_custom_call" | custom-call | flops 137438953472 | bytes 67108864 | tf_op jit(solution)/shard_map/pallas_call | solution.py:293
  379.7 1.3 copy.6

commit v4 on v3

--- a/solution.py
+++ b/solution.py
@@ -12,16 +12,18 @@
 
 MICRO_PER_ITEM = 2
 LOOKAHEAD = 4
+TAIL_ITEMS = 2
+TAIL_AHEAD = 2
 LAG_FINAL = 3
 COL_BLOCK = 512
-HEAD_FROM = 4
+HEAD_FROM = 5
 HEAD_FAR = 20
 HEAD_STEP = 3
 HEAD_KEEP = 1
 MID_DIAG = 3
-MID_FIRST = 47
-MID_STEP = 4
-LAST_DIAG = 2
+MID_FIRST = 46
+MID_STEP = 5
+LAST_DIAG = 4
 
 
 def mlp_kernel(dims, x_ref, gain_hbm, w1_hbm, w2_hbm, out_ref,
@@ -252,9 +254,11 @@
         def _():
             finish(t - LAG_FINAL)
 
-        @pl.when(t + LOOKAHEAD < work)
-        def _():
-            norm_and_send(t + LOOKAHEAD)
+        ahead = jnp.where((stage == 1) & (t + TAIL_AHEAD >= work - TAIL_ITEMS), TAIL_AHEAD, LOOKAHEAD)
+
+        @pl.when((t + ahead < work) & ((ahead == TAIL_AHEAD) | (stage == 0) | (t + LOOKAHEAD < work - TAIL_ITEMS)))
+        def _():
+            norm_and_send(t + ahead)
 
         @pl.when(t < work)
         def _():

time: 381 us -> 378 us (level)
  no operation moved by 1% of the time
where the time goes in v4:
time: 378 us
  Pallas kernels  377 us (100%)
    pallas_call x1, Pallas kernels, per_device(): pl.pallas_call(functools.partial(mlp_kernel, (items, rows, width, ring)),...  377 us

profile of v4, /device:TPU:4, one launch (start us, length us, event | category | flops | bytes accessed | tf_op | source)
XLA Modules:
  0.0 378.3 jit_solution(17432786344708681094)
XLA Ops:
  0.0 377.0 %shard_map.46 = bf16[16,32,2048]{2,1,0:T(8,128)(2,1)S(1)} custom-call(bf16[32,32,2048]{2,1,0:T(8,128)(2,1)} %bitcast.8, bf16[2,2048]{1,0:T(2,128)(2,1)} %bitcast.9, bf16[2,2048,2048]{2,1,0:T(8,128)(2,1)} %bitcast.6, bf16[2,2048,2048]{2,1,0:T(8,128)(2,1)} %bitcast.7), custom_call_target="tpu_custom_call" | custom-call | flops 137438953472 | bytes 67108864 | tf_op jit(solution)/shard_map/pallas_call | solution.py:297
  377.0 1.3 copy.6
